TPU v7x, 32 devices: a whole 2x2x4 slice. The times are simulated.
32 devices in a mesh: dp: 8 (over z, x), vocab: 4 (over y, core).
Axes of the slice: x: 2, y: 2, z: 4, core: 2. Of those that a mesh axis runs over, the one named last changes fastest.
Arguments:
- hidden_states: bfloat16 [1024, 3584], P('dp'), may hold values from -40 to 40
- head_weight: bfloat16 [3584, 98304], P(None, ('dp', 'vocab')), as said below
- target_ids: int32 [1024], replicated, may hold values from 0 to 98303
- seq_lengths: int32 [64], P('dp'), may hold values from 1 to 16
- domain_labels: int32 [64], P('dp'), may hold values from 0 to 21
- domain_weights: float32 [22], replicated, may hold values from 0.5 to 4
Outputs:
- token_loss: float32 [1024], P('dp')
- new_weights: float32 [22], replicated
Inputs may be any that keep to these rules, and one draw needn't show every extreme that they name: `head_weight`: every entry lies within 6 / sqrt(3584) of zero.
All inputs are finite; a program needn't handle non-finite values.
Results may differ from a plain program's by a relative error of at most 0.0003.
Values may be sent and summed in bfloat16 or wider, within the bound.
A program may use at most 128 MiB of HBM per device.

v0:
```python
import functools
import math

import jax
import jax.numpy as jnp
from jax import lax
from jax.experimental import pallas as pl
from jax.experimental.pallas import tpu as pltpu
from jax.sharding import PartitionSpec as P

SEQ_LEN = 16
DOMAINS = 22
LANES = 128
DOM_PAD = 24
CORES = 2

explore_share = 0.01
step_rate = 0.002


def nearest(p, i, n):
    if n == 2:
        return p if i == 0 else 1 - p
    m = jnp.minimum(p, n - 1 - p)
    k = (i + 1) // 2
    both = jnp.where(i % 2 == 1, p + k, p - k)
    far = i - m
    one = jnp.where(p + p <= n - 1, p + far, p - far)
    return jnp.where(i <= 2 * m, both, one)


def kernel(Z, X, Y, tok, cols, TN,
           hid_ref, w_ref, tgt_ref, len_ref, lab_ref, dw_ref,
           loss_ref, new_ref,
           buf, w_buf, m_ref, s_ref, p_ref, stat_out, stat_in, dom_out, dom_in,
           own_sem, w_sem, recv_sem, send_sem, st_send, st_recv, dm_send, dm_recv):
    nv = Y * CORES
    dp = Z * X
    ndev = dp * nv
    T = cols // TN
    M = X * tok
    pr = tok // nv
    me = lax.axis_index("dp")
    v = lax.axis_index("vocab")
    z, x = me // X, me % X
    y, c = v // CORES, v % CORES

    own_copy = pltpu.make_async_copy(hid_ref, buf.at[pl.ds(me * tok, tok)], own_sem)
    own_copy.start()

    def w_copy(j):
        return pltpu.make_async_copy(
            w_ref.at[:, pl.ds(pl.multiple_of(j * TN, TN), TN)], w_buf.at[j], w_sem.at[j]
        )

    for j in range(T):
        w_copy(j).start()

    def remote(kind, zs, xs, ys, cs, to):
        piece = ((zs * X + xs) * Y + ys) * CORES + cs
        rows = buf.at[pl.ds(pl.multiple_of(piece * pr, pr), pr)]
        return pltpu.make_async_remote_copy(
            src_ref=rows, dst_ref=rows,
            send_sem=send_sem.at[kind, piece], recv_sem=recv_sem.at[piece],
            device_id=to, device_id_type=pl.DeviceIdType.MESH,
        )

    def push(drain, cond, *what):
        def go():
            r = remote(*what)
            if drain:
                r.wait_send()
            else:
                r.start()
        if cond is None:
            go()
        else:
            pl.when(cond)(go)

    def dev(z_, x_, y_, c_):
        return (z_ * X + x_, y_ * CORES + c_)

    def arrive(drain, zs, xs, ys, cs):
        if not drain:
            remote(0, zs, xs, ys, cs, dev(z, x, y, 1 - c)).wait_recv()

    def line(drain, kind, n, pos, src, at, piece):
        up, down = pos + 1 < n, pos > 0
        if src is not None:
            if n == 2:
                return
            up, down = up & (src < pos), down & (src > pos)
        if n == 2:
            push(drain, None, kind, *piece, at(1 - pos))
            return
        push(drain, up, kind, *piece, at(pos + 1))
        push(drain, down, kind + 1, *piece, at(pos - 1))

    def send_z(drain, src, piece):
        line(drain, 1, Z, z, src, lambda q: dev(q, x, y, c), piece)

    def send_x(drain, src, piece):
        line(drain, 3, X, x, src, lambda q: dev(z, q, y, c), piece)

    def send_y(drain, src, piece):
        line(drain, 5, Y, y, src, lambda q: dev(z, x, q, c), piece)

    def send_c(drain, piece):
        push(drain, None, 0, *piece, dev(z, x, y, 1 - c))

    def y_first(i):
        return i == 0 or i == Z - 1

    def begin(drain):
        send_z(drain, None, (z, x, y, c))
        for k in range(Y):
            send_x(drain, None, (z, x, k, c))

    def z_step(drain, i):
        zs = nearest(z, i, Z)
        piece = (zs, x, y, c)
        arrive(drain, *piece)
        send_z(drain, zs, piece)
        send_y(drain, None, piece)
        send_x(drain, None, piece)
        send_c(drain, piece)

    def first_step(drain, i):
        zs = nearest(z, i, Z)
        if y_first(i):
            for t in range(1, Y):
                ys = nearest(y, t, Y)
                piece = (zs, x, ys, c)
                arrive(drain, *piece)
                send_y(drain, ys, piece)
                send_x(drain, None, piece)
                send_c(drain, piece)
        else:
            for t in range(1, X):
                xs = nearest(x, t, X)
                piece = (zs, xs, y, c)
                arrive(drain, *piece)
                send_x(drain, xs, piece)
                send_y(drain, None, piece)
                send_c(drain, piece)

    def second_step(drain, i):
        zs = nearest(z, i, Z)
        if y_first(i):
            for t in range(1, X):
                xs = nearest(x, t, X)
                for s in range(Y):
                    ys = nearest(y, s, Y)
                    piece = (zs, xs, ys, c)
                    arrive(drain, *piece)
                    send_x(drain, xs, piece)
                    send_c(drain, piece)
        else:
            for t in range(1, Y):
                ys = nearest(y, t, Y)
                for s in range(X):
                    xs = nearest(x, s, X)
                    piece = (zs, xs, ys, c)
                    arrive(drain, *piece)
                    send_y(drain, ys, piece)
                    send_c(drain, piece)

    def core_step(drain, i):
        zs = nearest(z, i, Z)
        for t in range(1 if i == 0 else 0, X):
            xs = nearest(x, t, X)
            for ys in range(Y):
                arrive(drain, zs, xs, ys, 1 - c)

    events = []
    for u in range(Z - 1):
        at = lambda twelfth: min(T - 1, twelfth * T // 12)
        if u == 0:
            events.append((0, at(0), first_step, 1))
            if Z > 3:
                events.append((0, at(2), z_step, 3))
            if Z > 2:
                events.append((0, at(6), first_step, 2))
        else:
            if u + 3 < Z:
                events.append((u, at(2), z_step, u + 3))
            if u + 2 < Z:
                events.append((u, at(3), first_step, u + 2))
        events.append((u, T - 1, second_step, u + 1))
        events.append((u, T - 1, core_step, u + 1))
    tile_events = [e for e in events if e[2] in (z_step, first_step)]
    end_events = [e for e in events if e[2] in (second_step, core_step)]

    own_copy.wait()
    begin(False)
    if Z > 1:
        z_step(False, 1)
    if Z > 2:
        z_step(False, 2)
    second_step(False, 0)
    core_step(False, 0)

    lane = lax.broadcasted_iota(jnp.int32, (M, LANES), 1)
    col_start = (me * nv + v) * cols

    def plane(u, _):
        zs = z if Z == 1 else nearest(z, u, Z) if Z != 2 else jnp.where(u == 0, z, 1 - z)
        r0 = pl.multiple_of(zs * M, M)
        m_ref[...] = jnp.full((M, LANES), -1e30, jnp.float32)
        s_ref[...] = jnp.zeros((M, LANES), jnp.float32)
        p_ref[...] = jnp.zeros((M, LANES), jnp.float32)

        def tile(j, _):
            for (eu, ej, fn, i) in tile_events:
                pl.when((u == eu) & (j == ej))(functools.partial(fn, False, i))

            @pl.when(u == 0)
            def _():
                w_copy(j).wait()

            logits = jnp.dot(buf[pl.ds(r0, M), :], w_buf[j], preferred_element_type=jnp.float32)
            off = tgt_ref[pl.ds(r0, M), :] - (col_start + j * TN) - lane
            m_old = m_ref[...]
            parts = [logits[:, g * LANES:(g + 1) * LANES] for g in range(TN // LANES)]
            m_new = m_old
            for a in parts:
                m_new = jnp.maximum(m_new, a)
            s = s_ref[...] * jnp.exp(m_old - m_new)
            pk = p_ref[...]
            for g, a in enumerate(parts):
                s = s + jnp.exp(a - m_new)
                pk = pk + jnp.where(off == g * LANES, a, 0.0)
            m_ref[...] = m_new
            s_ref[...] = s
            p_ref[...] = pk
            return 0

        lax.fori_loop(0, T, tile, 0)

        row_m = jnp.max(m_ref[...], axis=1, keepdims=True)
        row_s = jnp.sum(s_ref[...] * jnp.exp(m_ref[...] - row_m), axis=1, keepdims=True)
        row_p = jnp.sum(p_ref[...], axis=1, keepdims=True)
        packed = jnp.where(lane == 0, row_m, jnp.where(lane == 1, row_s, jnp.where(lane == 2, row_p, 0.0)))
        for xs in range(X):
            stat_out[zs * X + xs] = jnp.transpose(packed[xs * tok:(xs + 1) * tok])[:8]
        for xs in range(X):
            d = zs * X + xs

            @pl.when(d == me)
            def _():
                stat_in[me * nv + v] = stat_out[me]

            for k in range(nv):
                @pl.when((d != me) | (v != k))
                def _():
                    pltpu.make_async_remote_copy(
                        src_ref=stat_out.at[d], dst_ref=stat_in.at[me * nv + v],
                        send_sem=st_send, recv_sem=st_recv,
                        device_id=(d, k), device_id_type=pl.DeviceIdType.MESH,
                    ).start()
        for (eu, ej, fn, i) in end_events:
            pl.when(u == eu)(functools.partial(fn, False, i))
        return 0

    lax.fori_loop(0, Z, plane, 0)

    others = stat_in.at[pl.ds(0, ndev - 1)]
    pltpu.make_async_copy(others, others, st_recv).wait()
    ms = stat_in[:, 0, :]
    peak = jnp.max(ms, axis=0, keepdims=True)
    mass = jnp.sum(stat_in[:, 1, :] * jnp.exp(ms - peak), axis=0, keepdims=True)
    pick = jnp.sum(stat_in[:, 2, :], axis=0, keepdims=True)
    position = lax.broadcasted_iota(jnp.int32, (1, tok), 1) % SEQ_LEN
    valid = position < len_ref[...]
    loss = jnp.where(valid, jnp.log(mass) + peak - pick, 0.0)
    loss_ref[...] = loss
    dom = lax.broadcasted_iota(jnp.int32, (DOM_PAD, tok), 0)
    hot = dom == lab_ref[...]
    d_loss = jnp.sum(jnp.where(hot, loss, 0.0), axis=1, keepdims=True)
    d_count = jnp.sum(jnp.where(hot & valid, 1.0, 0.0), axis=1, keepdims=True)
    dlane = lax.broadcasted_iota(jnp.int32, (DOM_PAD, LANES), 1)
    dom_out[...] = jnp.where(dlane == 0, d_loss, jnp.where(dlane == 1, d_count, 0.0))
    dom_in[me] = dom_out[...]
    for k in range(1, dp):
        pltpu.make_async_remote_copy(
            src_ref=dom_out, dst_ref=dom_in.at[me],
            send_sem=dm_send, recv_sem=dm_recv,
            device_id=((me + k) % dp, v), device_id_type=pl.DeviceIdType.MESH,
        ).start()

    begin(True)
    if Z > 1:
        z_step(True, 1)
    if Z > 2:
        z_step(True, 2)
    second_step(True, 0)
    for (eu, ej, fn, i) in events:
        fn(True, i)
    pltpu.make_async_copy(others, others, st_send).wait()

    rest = dom_in.at[pl.ds(0, dp - 1)]
    pltpu.make_async_copy(rest, rest, dm_recv).wait()
    total = jnp.sum(dom_in[...], axis=0)
    dom_loss = jnp.sum(jnp.where(dlane == 0, total, 0.0), axis=1, keepdims=True)
    dom_count = jnp.sum(jnp.where(dlane == 1, total, 0.0), axis=1, keepdims=True)
    live = lax.broadcasted_iota(jnp.int32, (DOM_PAD, LANES), 0) < DOMAINS
    weights = jnp.where(live, dw_ref[...], 0.0)
    probability = (1.0 - DOMAINS * explore_share) * weights / jnp.sum(
        weights, axis=0, keepdims=True) + explore_share
    reward = dom_loss / jnp.maximum(dom_count, 1.0) / probability
    raised = jnp.where(live, weights * jnp.exp(step_rate * reward), 0.0)
    new_ref[...] = DOMAINS * raised / jnp.sum(raised, axis=0, keepdims=True)
    pltpu.make_async_copy(rest, rest, dm_send).wait()


def body(hidden_states, head_weight, target_ids, seq_lengths, domain_labels, domain_weights):
    tok, width = hidden_states.shape
    cols = head_weight.shape[1]
    dp = lax.axis_size("dp")
    nv = lax.axis_size("vocab")
    X = math.isqrt(dp // 2)
    Z = dp // X
    Y = nv // CORES
    tokens = dp * tok
    TN = 2 * LANES if cols % (2 * LANES) == 0 else LANES
    T = cols // TN
    M = X * tok
    tgt = jnp.broadcast_to(target_ids[:, None], (tokens, LANES))
    lens = jnp.repeat(seq_lengths, SEQ_LEN)[None, :]
    labs = jnp.repeat(domain_labels, SEQ_LEN)[None, :]
    dw = jnp.broadcast_to(
        jnp.concatenate([domain_weights, jnp.ones((DOM_PAD - DOMAINS,), jnp.float32)])[:, None],
        (DOM_PAD, LANES),
    )
    hbm = pl.BlockSpec(memory_space=pl.ANY)
    vmem = pl.BlockSpec(memory_space=pltpu.VMEM)
    f32 = jnp.float32
    dma = pltpu.SemaphoreType.DMA
    loss, new = pl.pallas_call(
        functools.partial(kernel, Z, X, Y, tok, cols, TN),
        out_shape=(jax.ShapeDtypeStruct((1, tok), f32), jax.ShapeDtypeStruct((DOM_PAD, LANES), f32)),
        in_specs=[hbm, hbm, vmem, vmem, vmem, vmem],
        out_specs=(vmem, vmem),
        scratch_shapes=[
            pltpu.VMEM((tokens, width), hidden_states.dtype),
            pltpu.VMEM((T, width, TN), head_weight.dtype),
            pltpu.VMEM((M, LANES), f32),
            pltpu.VMEM((M, LANES), f32),
            pltpu.VMEM((M, LANES), f32),
            pltpu.VMEM((dp, 8, tok), f32),
            pltpu.VMEM((dp * nv, 8, tok), f32),
            pltpu.VMEM((DOM_PAD, LANES), f32),
            pltpu.VMEM((dp, DOM_PAD, LANES), f32),
            dma(()),
            dma((T,)),
            dma((dp * nv,)),
            dma((7, dp * nv)),
            dma(()), dma(()), dma(()), dma(()),
        ],
        compiler_params=pltpu.CompilerParams(has_side_effects=True, vmem_limit_bytes=60 * 2**20),
    )(hidden_states, head_weight, tgt, lens, labs, dw)
    return loss[0], new[:DOMAINS, 0]


def solution(mesh):
    placed = (P("dp", None), P(None, ("dp", "vocab")), P(), P("dp"), P("dp"), P())
    return jax.shard_map(
        body, mesh=mesh, in_specs=placed, out_specs=(P("dp"), P()), check_vma=False
    )
```

profile of v0, /device:TPU:0, one launch (start us, length us, event | category | flops | bytes accessed | tf_op | source)
XLA Modules:
  0.0 104.4 jit_solution(15608727120045090219)
XLA Ops:
  0.6 0.7 concatenate.3
  1.3 0.7 broadcast_in_dim.9
  2.0 0.6 broadcast_in_dim_reshape.6.len_ref
  2.6 0.7 broadcast_in_dim.20
  3.3 0.6 broadcast_in_dim_reshape.7.lab_ref
  3.9 0.7 broadcast_in_dim.21.dw_ref
  4.6 1.7 %broadcast_in_dim.8.tgt_ref = s32[1024,128]{1,0:T(8,128)} broadcast(s32[1024]{0:T(1024)} %param.8), dimensions={0} | broadcast | bytes 528384 | tf_op jit(solution)/shard_map/broadcast_in_dim | solution.py:328
  6.3 95.7 %shard_map.77 = (f32[1,128]{1,0:T(1,128)}, f32[24,128]{1,0:T(8,128)}) custom-call(bf16[128,3584]{1,0:T(8,128)(2,1)} %hid_ref.1, bf16[3584,3072]{1,0:T(8,128)(2,1)} %w_ref.1, s32[1024,128]{1,0:T(8,128)} %broadcast_in_dim.8.tgt_ref, s32[1,128]{1,0:T(1,128)} %broadcast_in_dim_reshape.6.len_ref, s32[1,128]{1,0:T(1,128)} %broadcast_in_dim_reshape.7.lab_ref, ...), custom_call_target="tpu_custom_call" | custom-call | tf_op jit(solution)/shard_map/pallas_call | solution.py:339
  101.9 1.3 %slice_reduce_fusion = f32[22]{0:T(128)} fusion(f32[24,128]{1,0:T(8,128)} %get-tuple-element.5), kind=kLoop, calls=%fused_computation | loop fusion | bytes 176 | tf_op jit(solution)/shard_map/slice | solution.py:362
  103.3 1.2 %copy.9 = f32[128]{0:T(128)} copy(f32[128]{0:T(128)} %bitcast.1) | data formatting | bytes 1024
where the time goes:
time: 105 us; the launch traced here: 104 us
  Pallas kernels  95.7 us (91%)
  local copies, waits for them, and re-layouts  8.15 us (8%)
    pallas_call x1, Pallas kernels, body(): pl.pallas_call(functools.partial(kernel, Z, X, Y, tok, cols, TN), out_sha...  95.7 us

commit v1 on v0

v1 whole, which is shorter than its diff:
```python
import functools
import heapq
import math

import jax
import jax.numpy as jnp
from jax import lax
from jax.experimental import pallas as pl
from jax.experimental.pallas import tpu as pltpu
from jax.sharding import PartitionSpec as P

SEQ_LEN = 16
DOMAINS = 22
LANES = 128
DOM_PAD = 24
CORES = 2
LOW = -1e30
HALVES = 1

explore_share = 0.01
step_rate = 0.002


def nearest(p, i, n):
    if isinstance(p, int):
        q = min(p, n - 1 - p)
        k = (i + 1) // 2
        at = i if i > 2 * q else q + k if i % 2 else q - k
        return at if p == q else n - 1 - at
    if i == 0:
        return p
    if n == 2:
        return 1 - p
    q = jnp.minimum(p, n - 1 - p)
    k = (i + 1) // 2
    at = jnp.where(i > 2 * q, i, q + k if i % 2 else q - k)
    return jnp.where(p == q, at, n - 1 - at)


def y_first(i, Z):
    return i in YF or i == Z - 1


YF = (0, 1)
WIRE, LATE, CORE_LATE, TICK, FIRST, OWN_END, START = 4.92, 1.8, 1.4, 1.1, 3.0, 8.5, 2.0


def plan(Z, X, Y, H, TI):
    roles = range((Z + 1) // 2)
    if X != 2 or Y != 2:
        order = sorted(((i, t) for i in range(Z) for t in range(X)), key=lambda g: (2 * g[0] + 3 * g[1], g))
        steps = []
        for k, (i, t) in enumerate(order):
            if k:
                steps += [(k * TI, ("piece", i, t, s, h)) for s in range(Y) for h in range(H)]
                steps.append((k * TI, ("core", i, t)))
        return [(order, steps) for _ in roles]
    wire = WIRE / H
    rank = [{nearest(z, i, Z): i for i in range(Z)} for z in range(Z)]
    heap, count = [], [0]

    def post(at, *what):
        count[0] += 1
        heapq.heappush(heap, (at, count[0], what))

    free = {}

    def send(at, z, link, piece):
        zs, t, s, h = piece
        done = max(at, free.get((z, link), 0.0)) + wire
        free[z, link] = done
        to = {"up": z + 1, "down": z - 1}.get(link, z)
        post(done + LATE, "piece", to, (zs, t ^ (link == "x"), s ^ (link == "y"), h), link)

    def along(at, z, zs, piece):
        if z + 1 < Z and zs <= z:
            send(at, z, "up", piece)
        if z > 0 and zs >= z:
            send(at, z, "down", piece)

    inbox = [[] for _ in range(Z)]
    left = [{(i, t): 4 * H for i in range(Z) for t in range(2) if i or t} for _ in range(Z)]
    order = [[(0, 0)] for _ in range(Z)]
    steps = [[] for _ in range(Z)]
    tick, idle = [0] * Z, [False] * Z
    for z in range(Z):
        for h in range(H):
            along(START, z, z, (z, 0, 0, h))
            send(START, z, "x", (z, 0, 0, h))
        for h in range(H):
            send(START, z, "x", (z, 0, 1, h))
        post(FIRST, "free", z)

    def work(at, z):
        while inbox[z]:
            (zs, t, s, h), link = inbox[z].pop(0)
            i = rank[z][zs]
            steps[z].append((tick[z], ("piece", i, t, s, h)))
            piece = (zs, t, s, h)
            if link in ("up", "down"):
                along(at, z, zs, piece) if zs != z else None
                send(at, z, "y", piece)
                send(at, z, "x", piece)
            elif link == "y" and t == 0 and y_first(i, Z):
                send(at, z, "x", piece)
            elif link == "x" and s == 0 and i and not y_first(i, Z):
                send(at, z, "y", piece)
            left[z][i, t] -= 1
            post(at + CORE_LATE, "core", z, (i, t))
        n = tick[z]
        if n < TI:
            tick[z] += 1
            post(max(at + TICK, OWN_END * (n + 1) / TI), "free", z)
            return
        if n % TI == 0:
            ready = [g for g in left[z] if left[z][g] == 0 and g not in order[z]]
            if not ready:
                idle[z] = True
                return
            order[z].append(ready[0])
            steps[z].append((n, ("core",) + ready[0]))
        tick[z] += 1
        post(at + TICK, "free", z)

    while heap:
        at, _, what = heapq.heappop(heap)
        z = what[1]
        if what[0] == "piece":
            inbox[z].append(what[2:])
        elif what[0] == "core":
            left[z][what[2]] -= 1
        if what[0] == "free" or idle[z]:
            if len(order[z]) == 2 * Z and tick[z] == 2 * Z * TI:
                continue
            idle[z] = False
            work(at, z)
    return [(order[z], steps[z]) for z in roles]


def kernel(Z, X, Y, H, tok, cols, TN, U,
           hid_ref, w_ref, tgt_ref, len_ref, lab_ref, dw_ref,
           loss_ref, new_ref,
           buf, w_buf, lg, off_ref, m_ref, s_ref, p_ref,
           stat_out, stat_in, dom_out, dom_in,
           own_sem, w_sem, recv_sem, send_sem, st_send, st_recv, dm_send, dm_recv):
    nv = Y * CORES
    dp = Z * X
    ndev = dp * nv
    T = cols // TN
    TI = T // U
    NG = Z * X
    pr = tok // (nv * H)
    me = lax.axis_index("dp")
    v = lax.axis_index("vocab")
    z, x = me // X, me % X
    y, c = v // CORES, v % CORES

    own_copy = pltpu.make_async_copy(hid_ref, buf.at[pl.ds(pl.multiple_of(me * tok, tok), tok)], own_sem)
    own_copy.start()

    def w_copy(j):
        return pltpu.make_async_copy(
            w_ref.at[:, pl.ds(pl.multiple_of(j * TN, TN), TN)], w_buf.at[j], w_sem.at[j]
        )

    for j in range(T):
        w_copy(j).start()

    bar = pltpu.get_barrier_semaphore()
    for d in range(dp):
        for k in range(nv):
            @pl.when((d != me) | (v != k))
            def _():
                pl.semaphore_signal(bar, inc=1, device_id=(d, k), device_id_type=pl.DeviceIdType.MESH)

    def remote(kind, zs, xs, ys, cs, h, to):
        piece = (((zs * X + xs) * Y + ys) * CORES + cs) * H + h
        rows = buf.at[pl.ds(pl.multiple_of(piece * pr, pr), pr)]
        return pltpu.make_async_remote_copy(
            src_ref=rows, dst_ref=rows,
            send_sem=send_sem.at[kind, piece], recv_sem=recv_sem.at[piece],
            device_id=to, device_id_type=pl.DeviceIdType.MESH,
        )

    def push(drain, cond, *what):
        def go():
            r = remote(*what)
            if drain:
                r.wait_send()
            else:
                r.start()
        if cond is None:
            go()
        else:
            pl.when(cond)(go)

    def dev(z_, x_, y_, c_):
        return (z_ * X + x_, y_ * CORES + c_)

    def arrive(drain, zs, xs, ys, cs, h):
        if not drain:
            remote(0, zs, xs, ys, cs, h, dev(z, x, y, 1 - c)).wait_recv()

    def line(drain, kind, n, pos, src, at, piece):
        if n == 1:
            return
        up, down = pos + 1 < n, pos > 0
        if src is not None:
            if n == 2:
                return
            up, down = up & (src < pos), down & (src > pos)
        if n == 2:
            push(drain, None, kind, *piece, at(1 - pos))
            return
        push(drain, up, kind, *piece, at(pos + 1))
        push(drain, down, kind + 1, *piece, at(pos - 1))

    def send_z(drain, src, piece):
        line(drain, 1, Z, z, src, lambda q: dev(q, x, y, c), piece)

    def send_x(drain, src, piece):
        line(drain, 3, X, x, src, lambda q: dev(z, q, y, c), piece)

    def send_y(drain, src, piece):
        line(drain, 5, Y, y, src, lambda q: dev(z, x, q, c), piece)

    def send_c(drain, piece):
        push(drain, None, 0, *piece, dev(z, x, y, 1 - c))

    def begin(drain):
        for h in range(H):
            send_z(drain, None, (z, x, y, c, h))
            send_x(drain, None, (z, x, y, c, h))
        for k in range(1, Y):
            for h in range(H):
                send_x(drain, None, (z, x, nearest(y, k, Y), c, h))

    def piece_step(drain, i, t, s, h):
        zs, xs, ys = nearest(z, i, Z), nearest(x, t, X), nearest(y, s, Y)
        piece = (zs, xs, ys, c, h)
        arrive(drain, *piece)
        if t == 0 and s == 0:
            send_z(drain, zs, piece)
            send_y(drain, None, piece)
            send_x(drain, None, piece)
        elif t == 0:
            send_y(drain, ys, piece)
            if y_first(i, Z):
                send_x(drain, None, piece)
        elif s == 0:
            send_x(drain, xs, piece)
            if not y_first(i, Z):
                send_y(drain, None, piece)
        elif y_first(i, Z):
            send_x(drain, xs, piece)
        else:
            send_y(drain, ys, piece)
        send_c(drain, piece)

    def core_step(drain, i, t):
        zs, xs = nearest(z, i, Z), nearest(x, t, X)
        for ys in range(Y):
            for h in range(H):
                arrive(drain, zs, xs, ys, 1 - c, h)

    def run(drain, what):
        kind, *at = what
        (piece_step if kind == "piece" else core_step)(drain, *at)

    plans = plan(Z, X, Y, H, TI)
    role = jnp.minimum(z, Z - 1 - z)
    ids = [nearest(z, i, Z) * X + nearest(x, t, X) for i, t in plans[0][0]]
    for r in range(1, len(plans)):
        ids = [jnp.where(role == r, nearest(z, i, Z) * X + nearest(x, t, X), g)
               for (i, t), g in zip(plans[r][0], ids)]

    def take(q):
        def at_tick(whats):
            for what in whats:
                run(False, what)

        def of_role(steps):
            for at in sorted({at for at, _ in steps}):
                pl.when(q == at)(functools.partial(at_tick, [w for n, w in steps if n == at]))

        if all(p == plans[0] for p in plans):
            of_role(plans[0][1])
        else:
            for r, (_, steps) in enumerate(plans):
                pl.when(role == r)(functools.partial(of_role, steps))

    def group(k):
        g = ids[0]
        for n in range(1, NG):
            g = jnp.where(k == n, ids[n], g)
        return g

    col_start = (me * nv + v) * cols
    lane_t = lax.broadcasted_iota(jnp.int32, (LANES, LANES), 1)
    for g in range(dp * tok // LANES):
        rows = pl.ds(g * LANES, LANES)
        ids_row = jnp.broadcast_to(tgt_ref[g:g + 1, :], (LANES, LANES))
        off_ref[rows, :] = jnp.transpose(ids_row) - lane_t - col_start
    m_ref[...] = jnp.full(m_ref.shape, LOW, jnp.float32)
    s_ref[...] = jnp.zeros(s_ref.shape, jnp.float32)
    p_ref[...] = jnp.zeros(p_ref.shape, jnp.float32)
    lg[U - 1] = jnp.full((tok, TN), 3 * LOW, jnp.float32)

    pl.semaphore_wait(bar, ndev - 1)
    own_copy.wait()
    begin(False)

    def epilogue(slot, g, col):
        rows = pl.ds(pl.multiple_of(g * tok, tok), tok)
        off = off_ref[rows, :] - col
        m_old = m_ref[rows, :]
        parts = [lg[slot, :, n * LANES:(n + 1) * LANES] for n in range(TN // LANES)]
        m_new = m_old
        for a in parts:
            m_new = jnp.maximum(m_new, a)
        s = s_ref[rows, :] * jnp.exp(m_old - m_new)
        pk = p_ref[rows, :]
        for n, a in enumerate(parts):
            s = s + jnp.exp(a - m_new)
            pk = pk + jnp.where(off == n * LANES, a, 0.0)
        m_ref[rows, :] = m_new
        s_ref[rows, :] = s
        p_ref[rows, :] = pk

    row8 = lax.broadcasted_iota(jnp.int32, (8, tok), 0)

    def finish(g):
        rows = pl.ds(pl.multiple_of(g * tok, tok), tok)
        mt = jnp.transpose(m_ref[rows, :])
        st = jnp.transpose(s_ref[rows, :])
        pt = jnp.transpose(p_ref[rows, :])
        row_m = jnp.max(mt, axis=0, keepdims=True)
        row_s = jnp.sum(st * jnp.exp(mt - row_m), axis=0, keepdims=True)
        row_p = jnp.sum(pt, axis=0, keepdims=True)
        stat_out[g] = jnp.where(row8 == 0, row_m, jnp.where(row8 == 1, row_s, row_p))

        @pl.when(g == me)
        def _():
            stat_in[me * nv + v] = stat_out[me]

        for k in range(nv):
            @pl.when((g != me) | (v != k))
            def _():
                pltpu.make_async_remote_copy(
                    src_ref=stat_out.at[g], dst_ref=stat_in.at[me * nv + v],
                    send_sem=st_send, recv_sem=st_recv,
                    device_id=(g, k), device_id_type=pl.DeviceIdType.MESH,
                ).start()

    def tick(q, _):
        k = q // TI
        i = q - k * TI
        take(q)

        @pl.when(k == 0)
        def _():
            for u in range(U):
                w_copy(i * U + u).wait()

        @pl.when(((q - 1) % TI == 0) & (q > TI))
        def _():
            finish(group((q - 1) // TI - 1))

        g = group(k)
        rows = pl.ds(pl.multiple_of(g * tok, tok), tok)
        for u in range(U):
            j = i * U + u
            if u == 0:
                g_old = jnp.where(i == 0, group(jnp.maximum(k - 1, 0)), g)
                col = jnp.where(q == 0, -(1 << 30), jnp.where(i == 0, (T - 1) * TN, (j - 1) * TN))
                epilogue(U - 1, g_old, col)
            else:
                epilogue(u - 1, g, (j - 1) * TN)
            lg[u] = jnp.dot(buf[rows, :], w_buf[j], preferred_element_type=jnp.float32)
        return 0

    lax.fori_loop(0, NG * TI, tick, 0)
    epilogue(U - 1, ids[NG - 1], (T - 1) * TN)
    for k in range(NG):
        if (k + 1) * TI + 1 >= NG * TI:
            finish(ids[k])

    begin(True)
    for _, what in plans[0][1]:
        run(True, what)

    seq = lax.broadcasted_iota(jnp.int32, (1, tok), 1)
    lens = jnp.zeros((1, tok), jnp.int32)
    labs = jnp.zeros((1, tok), jnp.int32)
    for n in range(tok // SEQ_LEN):
        mine = seq // SEQ_LEN == n
        lens = jnp.where(mine, len_ref[n], lens)
        labs = jnp.where(mine, lab_ref[n], labs)
    dom_row = lax.broadcasted_iota(jnp.int32, (DOM_PAD, LANES), 0)
    live = dom_row < DOMAINS
    weights = jnp.zeros((DOM_PAD, LANES), jnp.float32)
    for n in range(DOMAINS):
        weights = jnp.where(dom_row == n, dw_ref[n], weights)
    probability = (1.0 - DOMAINS * explore_share) * weights / jnp.sum(
        weights, axis=0, keepdims=True) + explore_share

    others = stat_in.at[pl.ds(0, ndev - 1)]
    pltpu.make_async_copy(others, others, st_recv).wait()
    ms = stat_in[:, 0, :]
    peak = jnp.max(ms, axis=0, keepdims=True)
    mass = jnp.sum(stat_in[:, 1, :] * jnp.exp(ms - peak), axis=0, keepdims=True)
    pick = jnp.sum(stat_in[:, 2, :], axis=0, keepdims=True)
    valid = seq % SEQ_LEN < lens
    loss = jnp.where(valid, jnp.log(mass) + peak - pick, 0.0)
    loss_ref[...] = loss
    dom = lax.broadcasted_iota(jnp.int32, (DOM_PAD, tok), 0)
    hot = dom == labs
    d_loss = jnp.sum(jnp.where(hot, loss, 0.0), axis=1, keepdims=True)
    d_count = jnp.sum(jnp.where(hot & valid, 1.0, 0.0), axis=1, keepdims=True)
    dlane = lax.broadcasted_iota(jnp.int32, (DOM_PAD, LANES), 1)
    dom_out[...] = jnp.where(dlane == 0, d_loss, jnp.where(dlane == 1, d_count, 0.0))
    dom_in[me] = dom_out[...]
    for k in range(1, dp):
        pltpu.make_async_remote_copy(
            src_ref=dom_out, dst_ref=dom_in.at[me],
            send_sem=dm_send, recv_sem=dm_recv,
            device_id=((me + k) % dp, v), device_id_type=pl.DeviceIdType.MESH,
        ).start()
    pltpu.make_async_copy(others, others, st_send).wait()

    rest = dom_in.at[pl.ds(0, dp - 1)]
    pltpu.make_async_copy(rest, rest, dm_recv).wait()
    total = jnp.sum(dom_in[...], axis=0)
    dom_loss = jnp.sum(jnp.where(dlane == 0, total, 0.0), axis=1, keepdims=True)
    dom_count = jnp.sum(jnp.where(dlane == 1, total, 0.0), axis=1, keepdims=True)
    reward = dom_loss / jnp.maximum(dom_count, 1.0) / probability
    raised = jnp.where(live, weights * jnp.exp(step_rate * reward), 0.0)
    new_ref[...] = DOMAINS * raised / jnp.sum(raised, axis=0, keepdims=True)
    pltpu.make_async_copy(rest, rest, dm_send).wait()


def body(hidden_states, head_weight, target_ids, seq_lengths, domain_labels, domain_weights):
    tok, width = hidden_states.shape
    cols = head_weight.shape[1]
    dp = lax.axis_size("dp")
    nv = lax.axis_size("vocab")
    X = math.isqrt(dp // 2)
    Z = dp // X
    Y = nv // CORES
    tokens = dp * tok
    TN = next(n for n in (4 * LANES, 3 * LANES, 2 * LANES, LANES) if cols % n == 0)
    T = cols // TN
    U = 2 if T % 2 == 0 else 1
    H = HALVES if tok // (nv * HALVES) >= 16 else 1
    hbm = pl.BlockSpec(memory_space=pl.ANY)
    vmem = pl.BlockSpec(memory_space=pltpu.VMEM)
    smem = pl.BlockSpec(memory_space=pltpu.SMEM)
    f32 = jnp.float32
    dma = pltpu.SemaphoreType.DMA
    loss, new = pl.pallas_call(
        functools.partial(kernel, Z, X, Y, H, tok, cols, TN, U),
        out_shape=(jax.ShapeDtypeStruct((1, tok), f32), jax.ShapeDtypeStruct((DOM_PAD, LANES), f32)),
        in_specs=[hbm, hbm, vmem, smem, smem, smem],
        out_specs=(vmem, vmem),
        scratch_shapes=[
            pltpu.VMEM((tokens, width), hidden_states.dtype),
            pltpu.VMEM((T, width, TN), head_weight.dtype),
            pltpu.VMEM((U, tok, TN), f32),
            pltpu.VMEM((tokens, LANES), jnp.int32),
            pltpu.VMEM((tokens, LANES), f32),
            pltpu.VMEM((tokens, LANES), f32),
            pltpu.VMEM((tokens, LANES), f32),
            pltpu.VMEM((dp, 8, tok), f32),
            pltpu.VMEM((dp * nv, 8, tok), f32),
            pltpu.VMEM((DOM_PAD, LANES), f32),
            pltpu.VMEM((dp, DOM_PAD, LANES), f32),
            dma(()),
            dma((T,)),
            dma((dp * nv * H,)),
            dma((7, dp * nv * H)),
            dma(()), dma(()), dma(()), dma(()),
        ],
        compiler_params=pltpu.CompilerParams(
            has_side_effects=True, collective_id=0, vmem_limit_bytes=60 * 2**20),
    )(hidden_states, head_weight, target_ids.reshape(tokens // LANES, LANES), seq_lengths, domain_labels,
      domain_weights)
    return loss[0], new[:DOMAINS, 0]


def solution(mesh):
    placed = (P("dp", None), P(None, ("dp", "vocab")), P(), P("dp"), P("dp"), P())
    return jax.shard_map(
        body, mesh=mesh, in_specs=placed, out_specs=(P("dp"), P()), check_vma=False
    )
```

time: 105 us -> 73.4 us (0.70)
  Pallas kernels: 95.7 us -> 70.1 us
  local copies, waits for them, and re-layouts: 8.15 us -> 2.44 us
    pallas_call x1, Pallas kernels: 95.7 us -> 70.1 us  [body(): pl.pallas_call(functools.partial(kernel, Z, X, Y, H, tok, cols, TN, U), o...]
    broadcast_in_dim x4 -> x0, local copies, waits for them, and re-layouts: 3.79 us -> none  [the longest x1 1.68 us: body(): tgt = jnp.broadcast_to(target_ids[:, None], (tokens, LANES))]
    another operation x2 -> x0, local copies, waits for them, and re-layouts: 1.19 us -> none  [the longest x1 0.59 us: body(): lens = jnp.repeat(seq_lengths, SEQ_LEN)[None, :]]
where the time goes in v1:
time: 73.4 us; the launch traced here: 73.2 us
  Pallas kernels  70.1 us (96%)
  local copies, waits for them, and re-layouts  2.44 us (3%)
    pallas_call x1, Pallas kernels, body(): pl.pallas_call(functools.partial(kernel, Z, X, Y, H, tok, cols, TN, U), o...  70.1 us

profile of v1, /device:TPU:0, one launch (start us, length us, event | category | flops | bytes accessed | tf_op | source)
XLA Modules:
  0.0 73.2 jit_solution(15878785314469119873)
XLA Ops:
  0.6 70.1 %shard_map.77 = (f32[1,128]{1,0:T(1,128)}, f32[24,128]{1,0:T(8,128)}) custom-call(bf16[128,3584]{1,0:T(8,128)(2,1)} %hid_ref.1, bf16[3584,3072]{1,0:T(8,128)(2,1)} %w_ref.1, s32[8,128]{1,0:T(8,128)} %bitcast.2, s32[8]{0:T(128)} %len_ref.1, s32[8]{0:T(128)} %lab_ref.1, f32[22]{0:T(128)} %dw_ref.1), custom_call_target="tpu_custom_call" | custom-call | tf_op jit(solution)/shard_map/pallas_call | solution.py:460
  70.7 1.3 %slice_reduce_fusion = f32[22]{0:T(128)} fusion(f32[24,128]{1,0:T(8,128)} %get-tuple-element.5), kind=kLoop, calls=%fused_computation | loop fusion | bytes 176 | tf_op jit(solution)/shard_map/slice | solution.py:487
  72.1 1.1 %copy.9 = f32[128]{0:T(128)} copy(f32[128]{0:T(128)} %bitcast.3) | data formatting | bytes 1024

commit v2 on v1

--- a/solution.py
+++ b/solution.py
@@ -12,7 +12,6 @@
 SEQ_LEN = 16
 DOMAINS = 22
 LANES = 128
-DOM_PAD = 24
 CORES = 2
 LOW = -1e30
 HALVES = 1
@@ -42,7 +41,7 @@
 
 
 YF = (0, 1)
-WIRE, LATE, CORE_LATE, TICK, FIRST, OWN_END, START = 4.92, 1.8, 1.4, 1.1, 3.0, 8.5, 2.0
+WIRE, LATE, CORE_LATE, TICK, FIRST, OWN_END, START = 4.92, 2.2, 1.6, 1.14, 3.0, 9.0, 3.5
 
 
 def plan(Z, X, Y, H, TI):
@@ -139,10 +138,10 @@
 
 def kernel(Z, X, Y, H, tok, cols, TN, U,
            hid_ref, w_ref, tgt_ref, len_ref, lab_ref, dw_ref,
-           loss_ref, new_ref,
+           out_ref,
            buf, w_buf, lg, off_ref, m_ref, s_ref, p_ref,
            stat_out, stat_in, dom_out, dom_in,
-           own_sem, w_sem, recv_sem, send_sem, st_send, st_recv, dm_send, dm_recv):
+           own_sem, in_sem, w_sem, recv_sem, send_sem, st_send, st_recv, dm_send, dm_recv):
     nv = Y * CORES
     dp = Z * X
     ndev = dp * nv
@@ -164,14 +163,44 @@
         )
 
     for j in range(T):
-        w_copy(j).start()
+        w_copy(j).start(priority=1)
 
     bar = pltpu.get_barrier_semaphore()
-    for d in range(dp):
-        for k in range(nv):
-            @pl.when((d != me) | (v != k))
-            def _():
-                pl.semaphore_signal(bar, inc=1, device_id=(d, k), device_id_type=pl.DeviceIdType.MESH)
+
+    def signal(cond, sem, *at):
+        def go():
+            pl.semaphore_signal(sem, inc=1, device_id=(at[0] * X + at[1], at[2] * CORES + at[3]),
+                                device_id_type=pl.DeviceIdType.MESH)
+        if cond is None:
+            go()
+        else:
+            pl.when(cond)(go)
+        return 1 if cond is None else jnp.where(cond, 1, 0)
+
+    lines = ((Y, y, lambda q: (z, x, q, c)), (X, x, lambda q: (z, q, y, c)), (Z, z, lambda q: (q, x, y, c)))
+
+    def both(sem, n, pos, at):
+        return signal(pos + 1 < n, sem, *at(pos + 1)) + signal(pos > 0, sem, *at(pos - 1))
+
+    near = signal(None, bar, z, x, y, 1 - c)
+    for n, pos, at in lines:
+        near = near + both(bar, n, pos, at)
+
+    rounds = [None] + [line for line in lines for _ in range(line[0] - 1)]
+
+    def tell(r):
+        if rounds[r] is None:
+            return signal(None, in_sem.at[r], z, x, y, 1 - c)
+        return both(in_sem.at[r], *rounds[r])
+
+    def know(r):
+        n = 1
+        if rounds[r] is not None:
+            size, pos, _ = rounds[r]
+            n = jnp.where(pos + 1 < size, 1, 0) + jnp.where(pos > 0, 1, 0)
+        pl.semaphore_wait(in_sem.at[r], n)
+        if r + 1 < len(rounds):
+            tell(r + 1)
 
     def remote(kind, zs, xs, ys, cs, h, to):
         piece = (((zs * X + xs) * Y + ys) * CORES + cs) * H + h
@@ -306,9 +335,15 @@
     p_ref[...] = jnp.zeros(p_ref.shape, jnp.float32)
     lg[U - 1] = jnp.full((tok, TN), 3 * LOW, jnp.float32)
 
-    pl.semaphore_wait(bar, ndev - 1)
+    pl.semaphore_wait(bar, near)
     own_copy.wait()
     begin(False)
+    tell(0)
+    spread = 2 * TI >= len(rounds)
+
+    if not spread:
+        for r in range(len(rounds)):
+            know(r)
 
     def epilogue(slot, g, col):
         rows = pl.ds(pl.multiple_of(g * tok, tok), tok)
@@ -355,6 +390,9 @@
     def tick(q, _):
         k = q // TI
         i = q - k * TI
+        if spread:
+            for r in range(len(rounds)):
+                pl.when(q == r + 1)(functools.partial(know, r))
         take(q)
 
         @pl.when(k == 0)
@@ -396,13 +434,18 @@
         mine = seq // SEQ_LEN == n
         lens = jnp.where(mine, len_ref[n], lens)
         labs = jnp.where(mine, lab_ref[n], labs)
-    dom_row = lax.broadcasted_iota(jnp.int32, (DOM_PAD, LANES), 0)
-    live = dom_row < DOMAINS
-    weights = jnp.zeros((DOM_PAD, LANES), jnp.float32)
+    valid = seq % SEQ_LEN < lens
+    hot = lax.broadcasted_iota(jnp.int32, (LANES, tok), 0) == labs
+    d_count = jnp.sum(jnp.where(hot & valid, 1.0, 0.0), axis=1, keepdims=True)
+    dlane = lax.broadcasted_iota(jnp.int32, (LANES, LANES), 1)
+    counts = jnp.where(dlane == 1, d_count, 0.0)
+    dom = lax.broadcasted_iota(jnp.int32, (1, LANES), 1)
+    live = dom < DOMAINS
+    weights = jnp.zeros((1, LANES), jnp.float32)
     for n in range(DOMAINS):
-        weights = jnp.where(dom_row == n, dw_ref[n], weights)
+        weights = jnp.where(dom == n, dw_ref[n], weights)
     probability = (1.0 - DOMAINS * explore_share) * weights / jnp.sum(
-        weights, axis=0, keepdims=True) + explore_share
+        weights, axis=1, keepdims=True) + explore_share
 
     others = stat_in.at[pl.ds(0, ndev - 1)]
     pltpu.make_async_copy(others, others, st_recv).wait()
@@ -410,32 +453,25 @@
     peak = jnp.max(ms, axis=0, keepdims=True)
     mass = jnp.sum(stat_in[:, 1, :] * jnp.exp(ms - peak), axis=0, keepdims=True)
     pick = jnp.sum(stat_in[:, 2, :], axis=0, keepdims=True)
-    valid = seq % SEQ_LEN < lens
     loss = jnp.where(valid, jnp.log(mass) + peak - pick, 0.0)
-    loss_ref[...] = loss
-    dom = lax.broadcasted_iota(jnp.int32, (DOM_PAD, tok), 0)
-    hot = dom == labs
     d_loss = jnp.sum(jnp.where(hot, loss, 0.0), axis=1, keepdims=True)
-    d_count = jnp.sum(jnp.where(hot & valid, 1.0, 0.0), axis=1, keepdims=True)
-    dlane = lax.broadcasted_iota(jnp.int32, (DOM_PAD, LANES), 1)
-    dom_out[...] = jnp.where(dlane == 0, d_loss, jnp.where(dlane == 1, d_count, 0.0))
-    dom_in[me] = dom_out[...]
+    dom_out[...] = jnp.transpose(jnp.where(dlane == 0, d_loss, counts))[:8]
     for k in range(1, dp):
         pltpu.make_async_remote_copy(
             src_ref=dom_out, dst_ref=dom_in.at[me],
             send_sem=dm_send, recv_sem=dm_recv,
             device_id=((me + k) % dp, v), device_id_type=pl.DeviceIdType.MESH,
         ).start()
+    dom_in[me] = dom_out[...]
+    out_ref[0:1, :] = loss
     pltpu.make_async_copy(others, others, st_send).wait()
 
     rest = dom_in.at[pl.ds(0, dp - 1)]
     pltpu.make_async_copy(rest, rest, dm_recv).wait()
     total = jnp.sum(dom_in[...], axis=0)
-    dom_loss = jnp.sum(jnp.where(dlane == 0, total, 0.0), axis=1, keepdims=True)
-    dom_count = jnp.sum(jnp.where(dlane == 1, total, 0.0), axis=1, keepdims=True)
-    reward = dom_loss / jnp.maximum(dom_count, 1.0) / probability
+    reward = total[0:1] / jnp.maximum(total[1:2], 1.0) / probability
     raised = jnp.where(live, weights * jnp.exp(step_rate * reward), 0.0)
-    new_ref[...] = DOMAINS * raised / jnp.sum(raised, axis=0, keepdims=True)
+    out_ref[1:2, :] = DOMAINS * raised / jnp.sum(raised, axis=1, keepdims=True)
     pltpu.make_async_copy(rest, rest, dm_send).wait()
 
 
@@ -457,11 +493,11 @@
     smem = pl.BlockSpec(memory_space=pltpu.SMEM)
     f32 = jnp.float32
     dma = pltpu.SemaphoreType.DMA
-    loss, new = pl.pallas_call(
+    out = pl.pallas_call(
         functools.partial(kernel, Z, X, Y, H, tok, cols, TN, U),
-        out_shape=(jax.ShapeDtypeStruct((1, tok), f32), jax.ShapeDtypeStruct((DOM_PAD, LANES), f32)),
+        out_shape=jax.ShapeDtypeStruct((2, tok), f32),
         in_specs=[hbm, hbm, vmem, smem, smem, smem],
-        out_specs=(vmem, vmem),
+        out_specs=vmem,
         scratch_shapes=[
             pltpu.VMEM((tokens, width), hidden_states.dtype),
             pltpu.VMEM((T, width, TN), head_weight.dtype),
@@ -472,9 +508,10 @@
             pltpu.VMEM((tokens, LANES), f32),
             pltpu.VMEM((dp, 8, tok), f32),
             pltpu.VMEM((dp * nv, 8, tok), f32),
-            pltpu.VMEM((DOM_PAD, LANES), f32),
-            pltpu.VMEM((dp, DOM_PAD, LANES), f32),
+            pltpu.VMEM((8, LANES), f32),
+            pltpu.VMEM((dp, 8, LANES), f32),
             dma(()),
+            pltpu.SemaphoreType.REGULAR((1 + X + Y + Z - 3,)),
             dma((T,)),
             dma((dp * nv * H,)),
             dma((7, dp * nv * H)),
@@ -484,7 +521,7 @@
             has_side_effects=True, collective_id=0, vmem_limit_bytes=60 * 2**20),
     )(hidden_states, head_weight, target_ids.reshape(tokens // LANES, LANES), seq_lengths, domain_labels,
       domain_weights)
-    return loss[0], new[:DOMAINS, 0]
+    return out[0], out[1, :DOMAINS]
 
 
 def solution(mesh):

time: 73.4 us -> 67.3 us (0.917)
  Pallas kernels: 70.1 us -> 64.1 us
    pallas_call x1, Pallas kernels: 70.1 us -> 64.1 us  [body(): pl.pallas_call(functools.partial(kernel, Z, X, Y, H, tok, cols, TN, U), o...]
    squeeze x0 -> x2, local copies, waits for them, and re-layouts: none -> 2.38 us  [body(): return (out[0], out[1, :DOMAINS])]
    slice x1 -> x0, local copies, waits for them, and re-layouts: 1.33 us -> none  [body(): return (loss[0], new[:DOMAINS, 0])]
    unnamed x1 -> x0, local copies, waits for them, and re-layouts: 1.11 us -> none
where the time goes in v2:
time: 67.3 us; the launch traced here: 67.1 us
  Pallas kernels  64.1 us (95%)
  local copies, waits for them, and re-layouts  2.38 us (4%)
    pallas_call x1, Pallas kernels, body(): pl.pallas_call(functools.partial(kernel, Z, X, Y, H, tok, cols, TN, U), o...  64.1 us
    squeeze x2, local copies, waits for them, and re-layouts, body(): return (out[0], out[1, :DOMAINS])  2.38 us

profile of v2, /device:TPU:0, one launch (start us, length us, event | category | flops | bytes accessed | tf_op | source)
XLA Modules:
  0.0 67.1 jit_solution(1350714084275220450)
XLA Ops:
  0.6 64.1 %shard_map.77 = f32[2,128]{1,0:T(2,128)} custom-call(bf16[128,3584]{1,0:T(8,128)(2,1)} %hid_ref.1, bf16[3584,3072]{1,0:T(8,128)(2,1)} %w_ref.1, s32[8,128]{1,0:T(8,128)} %bitcast.5, s32[8]{0:T(128)} %len_ref.1, s32[8]{0:T(128)} %lab_ref.1, f32[22]{0:T(128)} %dw_ref.1), custom_call_target="tpu_custom_call" | custom-call | tf_op jit(solution)/shard_map/pallas_call | solution.py:496
  64.7 1.2 %slice_bitcast_fusion = f32[22]{0:T(128)} fusion(f32[2,128]{1,0:T(2,128)} %shard_map.77), kind=kLoop, calls=%fused_computation | loop fusion | bytes 176 | tf_op jit(solution)/shard_map/squeeze | solution.py:524
  65.9 1.2 %slice_bitcast_fusion.1 = f32[128]{0:T(128)} fusion(f32[2,128]{1,0:T(2,128)} %shard_map.77), kind=kLoop, calls=%fused_computation.1 | loop fusion | bytes 1024 | tf_op jit(solution)/shard_map/squeeze | solution.py:524

commit v3 on v2

--- a/solution.py
+++ b/solution.py
@@ -1,6 +1,7 @@
 import functools
 import heapq
 import math
+import random
 
 import jax
 import jax.numpy as jnp
@@ -36,74 +37,79 @@
     return jnp.where(p == q, at, n - 1 - at)
 
 
-def y_first(i, Z):
-    return i in YF or i == Z - 1
-
-
-YF = (0, 1)
 WIRE, LATE, CORE_LATE, TICK, FIRST, OWN_END, START = 4.92, 2.2, 1.6, 1.14, 3.0, 9.0, 3.5
-
-
-def plan(Z, X, Y, H, TI):
-    roles = range((Z + 1) // 2)
-    if X != 2 or Y != 2:
-        order = sorted(((i, t) for i in range(Z) for t in range(X)), key=lambda g: (2 * g[0] + 3 * g[1], g))
-        steps = []
-        for k, (i, t) in enumerate(order):
-            if k:
-                steps += [(k * TI, ("piece", i, t, s, h)) for s in range(Y) for h in range(H)]
-                steps.append((k * TI, ("core", i, t)))
-        return [(order, steps) for _ in roles]
-    wire = WIRE / H
+TRIES = 3000
+
+
+def far_first(Z, X, Y, H, TI):
+    order = sorted(((i, t) for i in range(Z) for t in range(X)), key=lambda g: (2 * g[0] + 3 * g[1], g))
+    steps = []
+    for k, (i, t) in enumerate(order):
+        if k:
+            steps += [(k * TI, ("piece", i, t, s, h)) for s in range(Y) for h in range(H)]
+            steps.append((k * TI, ("core", i, t)))
+    return order, steps
+
+
+def targets(Z, route, z, zs, t, s):
+    def inbound(w, t, s):
+        i = next(i for i in range(Z) if nearest(w, i, Z) == zs)
+        return route[min(w, Z - 1 - w)].get((i, t, s))
+
+    out = []
+    for w, link in ((z + 1, "up"), (z - 1, "down")):
+        if 0 <= w < Z and abs(w - zs) > abs(z - zs) and inbound(w, t, s) == "z":
+            out.append((link, w, (zs, t, s)))
+    if inbound(z, t, 1 - s) == "y":
+        out.append(("y", z, (zs, t, 1 - s)))
+    if inbound(z, 1 - t, s) == "x":
+        out.append(("x", z, (zs, 1 - t, s)))
+    return out
+
+
+def first_sends(Z, route, z):
+    return [(s, [e for e in targets(Z, route, z, z, 0, s) if e[0] != "y"]) for s in (0, 1)]
+
+
+def model(Z, H, TI, route):
     rank = [{nearest(z, i, Z): i for i in range(Z)} for z in range(Z)]
-    heap, count = [], [0]
+    onward = {(z, zs, t, s): targets(Z, route, z, zs, t, s)
+              for z in range(Z) for zs in range(Z) for t in (0, 1) for s in (0, 1)}
+    heap, free, got = [], {}, set()
+    count = [0]
 
     def post(at, *what):
         count[0] += 1
         heapq.heappush(heap, (at, count[0], what))
 
-    free = {}
-
-    def send(at, z, link, piece):
-        zs, t, s, h = piece
-        done = max(at, free.get((z, link), 0.0)) + wire
-        free[z, link] = done
-        to = {"up": z + 1, "down": z - 1}.get(link, z)
-        post(done + LATE, "piece", to, (zs, t ^ (link == "x"), s ^ (link == "y"), h), link)
-
-    def along(at, z, zs, piece):
-        if z + 1 < Z and zs <= z:
-            send(at, z, "up", piece)
-        if z > 0 and zs >= z:
-            send(at, z, "down", piece)
+    def send(at, z, link, to, piece):
+        free[z, link] = max(at, free.get((z, link), 0.0)) + WIRE / H
+        post(free[z, link] + LATE, "piece", to, piece)
 
     inbox = [[] for _ in range(Z)]
     left = [{(i, t): 4 * H for i in range(Z) for t in range(2) if i or t} for _ in range(Z)]
     order = [[(0, 0)] for _ in range(Z)]
     steps = [[] for _ in range(Z)]
-    tick, idle = [0] * Z, [False] * Z
+    tick, idle, end = [0] * Z, [False] * Z, [0.0] * Z
+    total = 2 * Z * TI
     for z in range(Z):
-        for h in range(H):
-            along(START, z, z, (z, 0, 0, h))
-            send(START, z, "x", (z, 0, 0, h))
-        for h in range(H):
-            send(START, z, "x", (z, 0, 1, h))
+        for s, sends in first_sends(Z, route, z):
+            for h in range(H):
+                for link, w, to in sends:
+                    send(START, z, link, w, to + (h,))
         post(FIRST, "free", z)
 
     def work(at, z):
         while inbox[z]:
-            (zs, t, s, h), link = inbox[z].pop(0)
+            piece = inbox[z].pop(0)
+            if (z, piece) in got:
+                return
+            got.add((z, piece))
+            zs, t, s, h = piece
             i = rank[z][zs]
             steps[z].append((tick[z], ("piece", i, t, s, h)))
-            piece = (zs, t, s, h)
-            if link in ("up", "down"):
-                along(at, z, zs, piece) if zs != z else None
-                send(at, z, "y", piece)
-                send(at, z, "x", piece)
-            elif link == "y" and t == 0 and y_first(i, Z):
-                send(at, z, "x", piece)
-            elif link == "x" and s == 0 and i and not y_first(i, Z):
-                send(at, z, "y", piece)
+            for link, w, to in onward[z, zs, t, s]:
+                send(at, z, link, w, to + (h,))
             left[z][i, t] -= 1
             post(at + CORE_LATE, "core", z, (i, t))
         n = tick[z]
@@ -119,21 +125,52 @@
             order[z].append(ready[0])
             steps[z].append((n, ("core",) + ready[0]))
         tick[z] += 1
+        end[z] = at + TICK
         post(at + TICK, "free", z)
 
     while heap:
         at, _, what = heapq.heappop(heap)
         z = what[1]
         if what[0] == "piece":
-            inbox[z].append(what[2:])
+            inbox[z].append(what[2])
         elif what[0] == "core":
             left[z][what[2]] -= 1
-        if what[0] == "free" or idle[z]:
-            if len(order[z]) == 2 * Z and tick[z] == 2 * Z * TI:
-                continue
+        if (what[0] == "free" or idle[z]) and tick[z] < total:
             idle[z] = False
             work(at, z)
-    return [(order[z], steps[z]) for z in roles]
+    full = all(n == total for n in tick)
+    return (round(max(end), 2) if full else 1e9, sum(end)), order, steps
+
+
+@functools.cache
+def plan(Z, H, TI):
+    roles = range((Z + 1) // 2)
+    best = []
+    for _ in roles:
+        links = {(0, 1, 0): "x", (0, 1, 1): "x"}
+        for i in range(1, Z):
+            last = "x" if i in (1, Z - 1) else "y"
+            links.update({(i, 0, 0): "z", (i, 0, 1): "y", (i, 1, 0): "x", (i, 1, 1): last})
+        best.append(links)
+    draw = random.Random(SEED)
+    at = best
+    score = at_score = model(Z, H, TI, best)[0]
+    for _ in range(TRIES):
+        trial = [dict(links) for links in at]
+        for _ in range(draw.choice((1, 1, 2, 3))):
+            links = draw.choice(trial)
+            key = draw.choice(sorted(links))
+            links[key] = draw.choice("xy" if key[0] == 0 else "zy" if key[1] == 0 else "zxy")
+        got = model(Z, H, TI, trial)[0]
+        if got <= at_score or draw.random() < math.exp(max(-60.0, (at_score[0] - got[0]) / 0.3)):
+            at, at_score = trial, got
+        if got < score:
+            best, score = trial, got
+    _, order, steps = model(Z, H, TI, best)
+    return best, order, steps
+
+
+SEED = 1
 
 
 def kernel(Z, X, Y, H, tok, cols, TN, U,
@@ -256,7 +293,34 @@
     def send_c(drain, piece):
         push(drain, None, 0, *piece, dev(z, x, y, 1 - c))
 
-    def begin(drain):
+    flat = X == 2 and Y == 2
+    roles = range((Z + 1) // 2) if flat else range(1)
+    role = jnp.minimum(z, Z - 1 - z)
+    if flat:
+        route, orders, all_steps = plan(Z, H, TI)
+    else:
+        order, steps = far_first(Z, X, Y, H, TI)
+        orders, all_steps = [order], [steps]
+
+    def by_links(drain, sends, piece):
+        low = z + z <= Z - 1
+        inward = jnp.where(low, 1, -1)
+        for link, _, _ in sends:
+            if link == "x":
+                push(drain, None, 3, *piece, dev(z, 1 - x, y, c))
+            elif link == "y":
+                push(drain, None, 5, *piece, dev(z, x, 1 - y, c))
+            elif link == "up":
+                push(drain, None, 1, *piece, dev(z + inward, x, y, c))
+            else:
+                push(drain, None, 2, *piece, dev(z - inward, x, y, c))
+
+    def begin(drain, r):
+        if flat:
+            for s, sends in first_sends(Z, route, r):
+                for h in range(H):
+                    by_links(drain, sends, (z, x, nearest(y, s, Y), c, h))
+            return
         for h in range(H):
             send_z(drain, None, (z, x, y, c, h))
             send_x(drain, None, (z, x, y, c, h))
@@ -264,59 +328,59 @@
             for h in range(H):
                 send_x(drain, None, (z, x, nearest(y, k, Y), c, h))
 
-    def piece_step(drain, i, t, s, h):
+    def piece_step(drain, r, i, t, s, h):
         zs, xs, ys = nearest(z, i, Z), nearest(x, t, X), nearest(y, s, Y)
         piece = (zs, xs, ys, c, h)
         arrive(drain, *piece)
-        if t == 0 and s == 0:
+        if flat:
+            by_links(drain, targets(Z, route, r, nearest(r, i, Z), t, s), piece)
+        elif t == 0 and s == 0:
             send_z(drain, zs, piece)
             send_y(drain, None, piece)
             send_x(drain, None, piece)
         elif t == 0:
             send_y(drain, ys, piece)
-            if y_first(i, Z):
-                send_x(drain, None, piece)
-        elif s == 0:
+            send_x(drain, None, piece)
+        else:
             send_x(drain, xs, piece)
-            if not y_first(i, Z):
-                send_y(drain, None, piece)
-        elif y_first(i, Z):
-            send_x(drain, xs, piece)
-        else:
-            send_y(drain, ys, piece)
         send_c(drain, piece)
 
-    def core_step(drain, i, t):
+    def core_step(drain, r, i, t):
         zs, xs = nearest(z, i, Z), nearest(x, t, X)
         for ys in range(Y):
             for h in range(H):
                 arrive(drain, zs, xs, ys, 1 - c, h)
 
-    def run(drain, what):
+    def run(drain, r, what):
         kind, *at = what
-        (piece_step if kind == "piece" else core_step)(drain, *at)
-
-    plans = plan(Z, X, Y, H, TI)
-    role = jnp.minimum(z, Z - 1 - z)
-    ids = [nearest(z, i, Z) * X + nearest(x, t, X) for i, t in plans[0][0]]
-    for r in range(1, len(plans)):
-        ids = [jnp.where(role == r, nearest(z, i, Z) * X + nearest(x, t, X), g)
-               for (i, t), g in zip(plans[r][0], ids)]
+        (piece_step if kind == "piece" else core_step)(drain, r, *at)
+
+    def by_role(what):
+        for r in roles:
+            if len(roles) == 1:
+                what(r)
+            else:
+                pl.when(role == r)(functools.partial(what, r))
+
+    ids = [nearest(z, i, Z) * X + nearest(x, t, X) for i, t in orders[0]]
+    for r in roles[1:]:
+        ids = [jnp.where(role == r, nearest(z, i, Z) * X + nearest(x, t, X), g) for (i, t), g in zip(orders[r], ids)]
 
     def take(q):
-        def at_tick(whats):
+        def at_tick(r, whats):
             for what in whats:
-                run(False, what)
-
-        def of_role(steps):
-            for at in sorted({at for at, _ in steps}):
-                pl.when(q == at)(functools.partial(at_tick, [w for n, w in steps if n == at]))
-
-        if all(p == plans[0] for p in plans):
-            of_role(plans[0][1])
-        else:
-            for r, (_, steps) in enumerate(plans):
-                pl.when(role == r)(functools.partial(of_role, steps))
+                run(False, r, what)
+
+        def of_role(r):
+            for at in sorted({at for at, _ in all_steps[r]}):
+                pl.when(q == at)(functools.partial(at_tick, r, [w for n, w in all_steps[r] if n == at]))
+
+        by_role(of_role)
+
+    def drain_role(r):
+        begin(True, r)
+        for _, what in all_steps[r]:
+            run(True, r, what)
 
     def group(k):
         g = ids[0]
@@ -337,7 +401,7 @@
 
     pl.semaphore_wait(bar, near)
     own_copy.wait()
-    begin(False)
+    by_role(functools.partial(begin, False))
     tell(0)
     spread = 2 * TI >= len(rounds)
 
@@ -423,9 +487,7 @@
         if (k + 1) * TI + 1 >= NG * TI:
             finish(ids[k])
 
-    begin(True)
-    for _, what in plans[0][1]:
-        run(True, what)
+    by_role(drain_role)
 
     seq = lax.broadcasted_iota(jnp.int32, (1, tok), 1)
     lens = jnp.zeros((1, tok), jnp.int32)

time: 67.3 us -> 65.9 us (0.979)
  Pallas kernels: 64.1 us -> 62.7 us
    pallas_call x1, Pallas kernels: 64.1 us -> 62.7 us  [body(): pl.pallas_call(functools.partial(kernel, Z, X, Y, H, tok, cols, TN, U), o...]
where the time goes in v3:
time: 65.9 us; the launch traced here: 65.7 us
  Pallas kernels  62.7 us (95%)
  local copies, waits for them, and re-layouts  2.38 us (4%)
    pallas_call x1, Pallas kernels, body(): pl.pallas_call(functools.partial(kernel, Z, X, Y, H, tok, cols, TN, U), o...  62.7 us
    squeeze x2, local copies, waits for them, and re-layouts, body(): return (out[0], out[1, :DOMAINS])  2.38 us

profile of v3, /device:TPU:0, one launch (start us, length us, event | category | flops | bytes accessed | tf_op | source)
XLA Modules:
  0.0 65.7 jit_solution(9088690895011068519)
XLA Ops:
  0.6 62.7 %shard_map.77 = f32[2,128]{1,0:T(2,128)} custom-call(bf16[128,3584]{1,0:T(8,128)(2,1)} %hid_ref.1, bf16[3584,3072]{1,0:T(8,128)(2,1)} %w_ref.1, s32[8,128]{1,0:T(8,128)} %bitcast.5, s32[8]{0:T(128)} %len_ref.1, s32[8]{0:T(128)} %lab_ref.1, f32[22]{0:T(128)} %dw_ref.1), custom_call_target="tpu_custom_call" | custom-call | tf_op jit(solution)/shard_map/pallas_call | solution.py:558
  63.3 1.2 %slice_bitcast_fusion = f32[22]{0:T(128)} fusion(f32[2,128]{1,0:T(2,128)} %shard_map.77), kind=kLoop, calls=%fused_computation | loop fusion | bytes 176 | tf_op jit(solution)/shard_map/squeeze | solution.py:586
  64.5 1.2 %slice_bitcast_fusion.1 = f32[128]{0:T(128)} fusion(f32[2,128]{1,0:T(2,128)} %shard_map.77), kind=kLoop, calls=%fused_computation.1 | loop fusion | bytes 1024 | tf_op jit(solution)/shard_map/squeeze | solution.py:586
